TPU v7x, 32 devices: a whole 2x2x4 slice. The times are simulated.
32 devices in a mesh: groups: 2 (over y), tensor: 4 (over z), frames: 4 (over x, core).
Axes of the slice: x: 2, y: 2, z: 4, core: 2. Of those that a mesh axis runs over, the one named last changes fastest.
Arguments:
- patches: bfloat16 [256, 16, 3072], P('tensor', ('groups', 'frames')), parts along dimension 1, may hold values from -12 to 12
- ln_gain: float32 [3072], replicated, may hold values from 0.5 to 1.5
- in_weight: bfloat16 [3072, 4, 768], P('frames', 'tensor'), may hold values from -0.109375 to 0.109375
- q_gain: float32 [4, 128], P('tensor'), may hold values from 0.1 to 1.9
- k_gain: float32 [4, 128], P('tensor'), may hold values from 0.1 to 1.9
- out_weight: bfloat16 [4, 512, 3072], P('tensor', None, 'frames'), may hold values from -0.25 to 0.25
Outputs:
- encoded: bfloat16 [256, 16, 3072], P('tensor', ('groups', 'frames')), parts along dimension 1
There are 2 independent parts, one for each index of `groups`. A program takes and returns all parts, laid end to end along the dimension named above; an argument that names none is the same for every part. Nothing has to cross between parts.
All inputs are finite; a program needn't handle non-finite values.
Results may differ from a plain program's by a relative error of at most 0.022.
Values may be sent and summed in bfloat16 or wider, within the bound.
No kernel may reach another device: no remote copies, remote signals or barrier semaphores. Data moves between devices by JAX's collectives and lax.ppermute only.
A program may use at most 64 MiB of HBM per device.

v0:
```python
import math
import jax
import jax.numpy as jnp
from jax import lax
from jax.sharding import PartitionSpec as P


def layer_norm(values, gain_vec):
    mean_val = jnp.mean(values, axis=-1, keepdims=True)
    centered = values - mean_val
    variance = jnp.mean(centered * centered, axis=-1, keepdims=True)
    return centered * lax.rsqrt(variance + 1e-06) * gain_vec


def local(patches, ln_gain, in_weight, q_gain, k_gain, out_weight):
    head_dim = q_gain.shape[1]
    normed = layer_norm(patches.astype(jnp.float32), ln_gain).astype(jnp.bfloat16)
    in_local = in_weight[:, 0, :]
    out_local = out_weight[0]
    every_patch = lax.all_gather(normed, "tensor", axis=0, tiled=True)
    joined_cols = jnp.einsum(
        "qye,ea->qya",
        every_patch,
        lax.all_gather(in_local, "frames", axis=0, tiled=True),
        preferred_element_type=jnp.float32,
    )
    query_slice = layer_norm(joined_cols[..., :head_dim], q_gain[0])
    key_slice = layer_norm(joined_cols[..., head_dim : 2 * head_dim], k_gain[0])
    value_slice = joined_cols[..., 2 * head_dim : 3 * head_dim]
    hidden = jax.nn.gelu(joined_cols[..., 3 * head_dim :], approximate=False)
    prepared = jnp.concatenate([query_slice, key_slice, value_slice, hidden], axis=-1).astype(
        jnp.bfloat16
    )
    query_slice = prepared[..., :head_dim]
    key_slice = prepared[..., head_dim : 2 * head_dim]
    value_slice = prepared[..., 2 * head_dim : 3 * head_dim]
    attention_logits = jnp.einsum(
        "ldg,bdg->dlb", query_slice, key_slice, preferred_element_type=jnp.float32
    ) * (1.0 / math.sqrt(head_dim))
    exponent_scores = jnp.exp(attention_logits)
    softmax_total = jnp.sum(exponent_scores, axis=-1)
    attention_output = jnp.einsum(
        "jdl,ljg->djg",
        exponent_scores.astype(jnp.bfloat16),
        value_slice,
        preferred_element_type=jnp.float32,
    )
    attention_output = attention_output / jnp.transpose(softmax_total)[:, :, None]
    blended_rows = jnp.concatenate(
        [attention_output.astype(jnp.bfloat16), prepared[..., 3 * head_dim :]], axis=-1
    )
    combined_output = lax.all_gather(out_local, "frames", axis=1, tiled=True)
    summed = lax.psum_scatter(
        jnp.einsum(
            "vto,ox->vtx", blended_rows, combined_output, preferred_element_type=jnp.float32
        ).astype(jnp.bfloat16),
        "tensor",
        scatter_dimension=0,
        tiled=True,
    ).astype(jnp.float32)
    return (patches.astype(jnp.float32) + summed).astype(jnp.bfloat16)


def solution(mesh):
    return jax.shard_map(
        local,
        mesh=mesh,
        in_specs=(
            P("tensor", ("groups", "frames"), None),
            P(),
            P("frames", "tensor", None),
            P("tensor", None),
            P("tensor", None),
            P("tensor", None, "frames"),
        ),
        out_specs=P("tensor", ("groups", "frames"), None),
        check_vma=False,
    )
```

profile of v0, /device:TPU:0, one launch (start us, length us, event | category | flops | bytes accessed | tf_op | source)
XLA Modules:
  0.0 220.3 jit_solution(9089769881547310153)
XLA Ops:
  6.5 1.4 convert_reduce_fusion
  7.9 1.5 fusion.5
  9.5 1.2 fusion.7
  10.7 0.0 all-gather.6.cloned.1.call-update
  10.7 0.0 all-gather.8.cloned.1.call-start
  10.8 0.7 all-gather.8.cloned.1.call-update
  11.5 0.0 all-gather.10.cloned.1.call-start
  11.5 0.7 all-gather.10.cloned.1.call-update
  12.2 0.0 copy-start.2
  12.2 0.0 reduce-scatter.2.cloned.1.call-start
  12.3 64.8 %all-gather.6.cloned.1.call-done = bf16[256,2,3072]{2,0,1:T(8,128)(2,1)} async-done(((bf16[64,2,3072]{2,0,1:T(8,128)(2,1)}), bf16[256,2,3072]{2,0,1:T(8,128)(2,1)}) %all-gather.6.cloned.1.call-update) | async-done | bytes 3145744 | tf_op jit(solution)/shard_map/all_gather | solution.py:20
  77.0 37.7 %all-gather.8.cloned.1.call-done = bf16[3072,1,768]{2,0,1:T(8,128)(2,1)} async-done(((bf16[768,1,768]{2,0,1:T(8,128)(2,1)}), bf16[3072,1,768]{2,0,1:T(8,128)(2,1)}) %all-gather.8.cloned.1.call-update) | async-done | bytes 4718608 | tf_op jit(solution)/shard_map/all_gather | solution.py:24
  114.7 5.9 %fusion = f32[256,2,768]{2,0,1:T(8,128)S(1)} fusion(bf16[256,2,3072]{2,0,1:T(8,128)(2,1)} %all-gather.6.cloned.1.call-done, bf16[3072,1,768]{2,0,1:T(8,128)(2,1)} %all-gather.8.cloned.1.call-done), kind=kOutput, calls=%fused_computation | convolution fusion | flops 2415919104 | bytes 9437184 | tf_op jit(solution)/shard_map/qye,ea->qya/dot_general | solution.py:21
  120.6 0.2 slice_reduce_fusion.1
  120.8 0.4 multiply_reduce_fusion.1
  121.3 0.5 fusion.33
  121.8 0.3 fusion.11
  122.0 1.7 fusion.14
  123.8 21.1 %all-gather.10.cloned.1.call-done = bf16[1,512,3072]{2,1,0:T(8,128)(2,1)} async-done(((bf16[1,512,768]{2,1,0:T(8,128)(2,1)}), bf16[1,512,3072]{2,1,0:T(8,128)(2,1)}) %all-gather.10.cloned.1.call-update) | async-done | bytes 3145744 | tf_op jit(solution)/shard_map/all_gather | solution.py:52
  144.8 5.4 %convolution_convert_fusion = bf16[256,2,3072]{2,0,1:T(8,128)(2,1)} fusion(bf16[1,512,3072]{2,1,0:T(8,128)(2,1)} %all-gather.10.cloned.1.call-done, bf16[256,2,384]{2,0,1:T(8,128)(2,1)S(1)} %fusion.14, bf16[256,2,128]{2,0,1:T(8,128)(2,1)S(1)} %fusion.11), kind=kOutput, calls=%fused_computation.2 | convolution fusion | flops 1613234176 | bytes 6815744 | tf_op jit(solution)/shard_map/vto,ox->vtx/dot_general | solution.py:54
  150.2 0.0 reduce-scatter.2.cloned.1.call-update
  150.2 60.6 %reduce-scatter.2.cloned.1.call-done = bf16[64,2,3072]{2,0,1:T(8,128)(2,1)} async-done(((bf16[256,2,3072]{2,0,1:T(8,128)(2,1)}), bf16[64,2,3072]{2,0,1:T(8,128)(2,1)}) %reduce-scatter.2.cloned.1.call-update) | async-done | bytes 786448 | tf_op jit(solution)/shard_map/reduce_scatter | solution.py:53
  210.8 1.3 fusion.8
  212.1 1.7 copy.8
  (13 shorter events, 0.1 us)
Async XLA Ops:
  6.5 2.9 %copy-start = (bf16[64,2,3072]{2,1,0:T(2,128)(2,1)S(1)}, bf16[64,2,3072]{2,1,0:T(2,128)(2,1)}, u32[]{:S(2)}) copy-start(bf16[64,2,3072]{2,1,0:T(2,128)(2,1)} %param.6) | copy-start | bytes 2359300
  6.5 2.9 %copy-start.1 = (f32[3072]{0:T(1024)S(1)}, f32[3072]{0:T(1024)}, u32[]{:S(2)}) copy-start(f32[3072]{0:T(1024)} %param.7) | copy-start | bytes 36868
  6.5 70.5 %all-gather.6.cloned.1.call-start = ((), (), s32[]{:S(2)}) async-start(), calls=%async_computation.1 | async-start | bytes 3932160 | tf_op jit(solution)/shard_map/all_gather | solution.py:20
  10.7 104.0 %all-gather.8.cloned.1.call-start = ((), (), s32[]{:S(2)}) async-start(), calls=%async_computation.3 | async-start | bytes 5898240 | tf_op jit(solution)/shard_map/all_gather | solution.py:24
  11.5 133.3 %all-gather.10.cloned.1.call-start = ((), (), s32[]{:S(2)}) async-start(), calls=%async_computation.4 | async-start | bytes 3932160 | tf_op jit(solution)/shard_map/all_gather | solution.py:52
  12.2 109.0 %copy-start.2 = (f32[1,128]{1,0:T(1,128)S(1)}, f32[1,128]{1,0:T(1,128)}, u32[]{:S(2)}) copy-start(f32[1,128]{1,0:T(1,128)} %param.10) | copy-start | bytes 1540
  12.2 109.0 %copy-start.3 = (f32[1,128]{1,0:T(1,128)S(1)}, f32[1,128]{1,0:T(1,128)}, u32[]{:S(2)}) copy-start(f32[1,128]{1,0:T(1,128)} %param.9) | copy-start | bytes 1540
  12.2 198.5 %reduce-scatter.2.cloned.1.call-start = ((), (), s32[]{:S(2)}) async-start(), calls=%async_computation.2 | async-start | bytes 3932160 | tf_op jit(solution)/shard_map/reduce_scatter | solution.py:53
Sparse Core Ops, SparseCore 0:
  10.8 66.1 all-gather.5
  78.6 36.0 all-gather.7
  116.3 28.5 all-gather.9
  150.3 60.3 reduce-scatter.1
where the time goes:
time: 221 us; the launch traced here: 220 us
  waiting for transfers between devices  185 us (84%)
  between operations  13.2 us (6%)
  matrix products  12 us (5%)
  other arithmetic  7.81 us (4%)
    all_gather x1, waiting for transfers between devices, local(): every_patch = lax.all_gather(normed, 'tensor', axis=0, tiled=True)  64.8 us
    reduce_scatter x1, waiting for transfers between devices, local(): lax.psum_scatter(jnp.einsum('vto,ox->vtx', blended_rows, combined_output,...  60.6 us
    all_gather x1, waiting for transfers between devices, local(): lax.all_gather(in_local, 'frames', axis=0, tiled=True)  37.7 us
    all_gather x1, waiting for transfers between devices, local(): combined_output = lax.all_gather(out_local, 'frames', axis=1, tiled=True)  21.1 us
    dot_general x1, matrix products, local(): jnp.einsum('qye,ea->qya', every_patch, lax.all_gather(in_local, 'frames',...  5.89 us
    dot_general x1, matrix products, local(): jnp.einsum('vto,ox->vtx', blended_rows, combined_output, preferred_elemen...  5.36 us
  transfers between devices with their start and end apart: 4, of which 4 were waited for; matrix products, arithmetic and copies ran while one was open for 4% of the time, Pallas kernels for 0%

commit v1 on v0

--- a/solution.py
+++ b/solution.py
@@ -3,6 +3,31 @@
 import jax.numpy as jnp
 from jax import lax
 from jax.sharding import PartitionSpec as P
+
+
+def joined_along(parts, dim):
+    parts = jnp.moveaxis(parts, 0, dim)
+    shape = parts.shape
+    return parts.reshape(*shape[:dim], shape[dim] * shape[dim + 1], *shape[dim + 2 :])
+
+
+def on_each_block(value, axis, dim, apply, out_dim):
+    devices, mine, span = (lax.axis_size(axis), lax.axis_index(axis), value.shape[dim])
+    forward = [(i, (i + 1) % devices) for i in range(devices)]
+    downward = [(i, (i - 1) % devices) for i in range(devices)]
+    half = devices // 2
+    pieces = {}
+    from_left = from_right = value
+    for turn in range(half + 1):
+        next_left = lax.ppermute(from_left, axis, forward) if turn < half else None
+        next_right = lax.ppermute(from_right, axis, downward) if turn < devices - half - 1 else None
+        pieces[-turn] = apply(from_left, (mine - turn) % devices * span)
+        if 0 < turn < devices - half:
+            pieces[turn] = apply(from_right, (mine + turn) % devices * span)
+        from_left, from_right = (next_left, next_right)
+    pieces = jnp.stack([pieces[k] for k in sorted(pieces)])
+    pieces = pieces[(jnp.arange(devices) - mine + half) % devices]
+    return joined_along(pieces, out_dim)
 
 
 def layer_norm(values, gain_vec):
@@ -49,10 +74,15 @@
     blended_rows = jnp.concatenate(
         [attention_output.astype(jnp.bfloat16), prepared[..., 3 * head_dim :]], axis=-1
     )
-    combined_output = lax.all_gather(out_local, "frames", axis=1, tiled=True)
     summed = lax.psum_scatter(
-        jnp.einsum(
-            "vto,ox->vtx", blended_rows, combined_output, preferred_element_type=jnp.float32
+        on_each_block(
+            out_local,
+            "frames",
+            1,
+            lambda own_block, at: jnp.einsum(
+                "vto,ox->vtx", blended_rows, own_block, preferred_element_type=jnp.float32
+            ),
+            2,
         ).astype(jnp.bfloat16),
         "tensor",
         scatter_dimension=0,

time: 221 us -> 203 us (0.919)
  waiting for transfers between devices: 185 us -> 159 us
  local copies, waits for them, and re-layouts: 1.71 us -> 8.15 us
  starting transfers between devices: 0.12 us -> 5.06 us
  matrix products: 12 us -> 8.99 us
    all_gather x1 -> x0, waiting for transfers between devices: 21.1 us -> none  [local(): combined_output = lax.all_gather(out_local, 'frames', axis=1, tiled=True)]
    all_gather x1, waiting for transfers between devices: 64.8 us -> 45.1 us  [local(): every_patch = lax.all_gather(normed, 'tensor', axis=0, tiled=True)]
    ppermute x0 -> x3, waiting for transfers between devices: none -> 15.4 us  [the longest x2 15.4 us: on_each_block(): next_left = lax.ppermute(from_left, axis, forward) if turn < half else None]
    ppermute x0 -> x3, starting transfers between devices: none -> 4.98 us  [the longest x2 3 us: on_each_block(): next_left = lax.ppermute(from_left, axis, forward) if turn < half else None]
    convert_element_type x0 -> x1, local copies, waits for them, and re-layouts: none -> 3.98 us  [local(): summed = lax.psum_scatter(on_each_block(out_local, 'frames', 1, lambda ow...]
    dot_general x1 -> x4, matrix products: 5.36 us -> 2.33 us  [local(): jnp.einsum('vto,ox->vtx', blended_rows, own_block, preferred_element_type...]
    gather x0 -> x1, local copies, waits for them, and re-layouts: none -> 2.45 us  [on_each_block(): pieces = pieces[(jnp.arange(devices) - mine + half) % devices]]
  transfers between devices with their start and end apart: 4 -> 6, of which waited for: 4 -> 4; matrix products, arithmetic and copies ran while one was open for 4% -> 5% of each run, Pallas kernels for 0% -> 0%
where the time goes in v1:
time: 203 us
  waiting for transfers between devices  159 us (78%)
  between operations  13.3 us (7%)
  matrix products  8.99 us (4%)
  other arithmetic  8.27 us (4%)
  local copies, waits for them, and re-layouts  8.15 us (4%)
  starting transfers between devices  5.06 us (2%)
    reduce_scatter x1, waiting for transfers between devices, local(): lax.psum_scatter(on_each_block(out_local, 'frames', 1, lambda own_block,...  60.6 us
    all_gather x1, waiting for transfers between devices, local(): every_patch = lax.all_gather(normed, 'tensor', axis=0, tiled=True)  45.1 us
    all_gather x1, waiting for transfers between devices, local(): lax.all_gather(in_local, 'frames', axis=0, tiled=True)  37.7 us
    ppermute x2, waiting for transfers between devices, on_each_block(): next_left = lax.ppermute(from_left, axis, forward) if turn < half else None  15.4 us
    dot_general x1, matrix products, local(): jnp.einsum('qye,ea->qya', every_patch, lax.all_gather(in_local, 'frames',...  5.89 us
  transfers between devices with their start and end apart: 6, of which 4 were waited for; matrix products, arithmetic and copies ran while one was open for 5% of the time, Pallas kernels for 0%

profile of v1, /device:TPU:0, one launch (start us, length us, event | category | flops | bytes accessed | tf_op | source)
XLA Modules:
  0.0 203.2 jit_solution(2506508884416657072)
XLA Ops:
  6.5 1.4 convert_reduce_fusion
  7.9 1.5 fusion.4
  9.5 1.2 fusion.6
  10.8 0.7 all-gather.6.cloned.1.call-update
  11.5 0.5 collective-permute-start
  12.1 2.0 collective-permute-start.2
  14.1 15.4 %collective-permute-done = bf16[512,768]{1,0:T(8,128)(2,1)S(1)} collective-permute-done((bf16[512,768]{1,0:T(8,128)(2,1)S(1)}, bf16[512,768]{1,0:T(8,128)(2,1)S(1)}, u32[]{:S(2)}, u32[]{:S(2)}) %collective-permute-start) | collective-permute-done | bytes 786464 | tf_op jit(solution)/shard_map/ppermute | solution.py:22
  29.5 2.5 %collective-permute-start.1 = (bf16[512,768]{1,0:T(8,128)(2,1)S(1)}, bf16[512,768]{1,0:T(8,128)(2,1)S(1)}, u32[]{:S(2)}, u32[]{:S(2)}) collective-permute-start(bf16[512,768]{1,0:T(8,128)(2,1)S(1)} %collective-permute-done), channel_id=1, source_target_pairs={{0,1},{1,2},{2,3},{3,0},{4,5},{5,6},{6,7},{7,4},{8,9},{9,10},{10,1... | collective-permute-start | bytes 2359304 | tf_op jit(solution)/shard_map/ppermute | solution.py:22
  32.0 45.1 %all-gather.4.cloned.1.call-done = bf16[256,2,3072]{2,0,1:T(8,128)(2,1)} async-done(((bf16[64,2,3072]{2,0,1:T(8,128)(2,1)}), bf16[256,2,3072]{2,0,1:T(8,128)(2,1)}) %all-gather.4.cloned.1.call-update) | async-done | bytes 3145744 | tf_op jit(solution)/shard_map/all_gather | solution.py:45
  77.1 37.7 %all-gather.6.cloned.1.call-done = bf16[3072,1,768]{2,0,1:T(8,128)(2,1)} async-done(((bf16[768,1,768]{2,0,1:T(8,128)(2,1)}), bf16[3072,1,768]{2,0,1:T(8,128)(2,1)}) %all-gather.6.cloned.1.call-update) | async-done | bytes 4718608 | tf_op jit(solution)/shard_map/all_gather | solution.py:49
  114.7 5.9 %fusion = f32[256,2,768]{2,0,1:T(8,128)S(1)} fusion(bf16[256,2,3072]{2,0,1:T(8,128)(2,1)} %all-gather.4.cloned.1.call-done, bf16[3072,1,768]{2,0,1:T(8,128)(2,1)} %all-gather.6.cloned.1.call-done), kind=kOutput, calls=%fused_computation.2 | convolution fusion | flops 2415919104 | bytes 9437184 | tf_op jit(solution)/shard_map/qye,ea->qya/dot_general | solution.py:46
  120.9 1.7 fusion.13
  122.6 0.4 multiply_reduce_fusion.1
  123.0 0.5 fusion.34
  123.8 0.6 convolution_bitcast_fusion.1
  124.4 0.6 convolution_bitcast_fusion.2
  125.0 0.6 convolution_bitcast_fusion.3
  125.6 0.6 convolution_bitcast_fusion
  126.2 0.4 pad_maximum_fusion
  126.6 2.5 %gather_fusion = bf16[4,256,2,768]{3,1,2,0:T(8,128)(2,1)} fusion(bf16[4,256,2,768]{3,1,2,0:T(8,128)(2,1)S(1)} %pad_maximum_fusion, s32[1024]{0:T(1024)S(1)} %pad_clamp_fusion), kind=kCustom, calls=%fused_computation | custom fusion | bytes 6291472 | tf_op jit(solution)/shard_map/gather | solution.py:29
  129.1 4.0 %copy.16 = bf16[4,2,32,8,768]{4,3,0,2,1:T(8,128)(2,1)} copy(bf16[4,2,32,8,768]{4,3,2,1,0:T(8,128)(2,1)} %bitcast.44) | data formatting | bytes 6291456 | tf_op jit(solution)/shard_map/convert_element_type | solution.py:86
  133.1 60.6 %reduce-scatter.2.cloned.1.call-done = bf16[64,2,3072]{2,0,1:T(8,128)(2,1)} async-done(((bf16[256,2,3072]{2,0,1:T(8,128)(2,1)}), bf16[64,2,3072]{2,0,1:T(8,128)(2,1)}) %reduce-scatter.2.cloned.1.call-update) | async-done | bytes 786448 | tf_op jit(solution)/shard_map/reduce_scatter | solution.py:77
  193.6 1.3 fusion.7
  195.0 1.7 copy.12
  (28 shorter events, 0.7 us)
Async XLA Ops:
  6.5 2.9 %copy-start = (bf16[64,2,3072]{2,1,0:T(2,128)(2,1)S(1)}, bf16[64,2,3072]{2,1,0:T(2,128)(2,1)}, u32[]{:S(2)}) copy-start(bf16[64,2,3072]{2,1,0:T(2,128)(2,1)} %param.6) | copy-start | bytes 2359300
  6.5 2.9 %copy-start.2 = (f32[3072]{0:T(1024)S(1)}, f32[3072]{0:T(1024)}, u32[]{:S(2)}) copy-start(f32[3072]{0:T(1024)} %param.7) | copy-start | bytes 36868
  6.5 70.5 %all-gather.4.cloned.1.call-start = ((), (), s32[]{:S(2)}) async-start(), calls=%async_computation.1 | async-start | bytes 3932160 | tf_op jit(solution)/shard_map/all_gather | solution.py:45
  9.5 2.1 %copy-start.3 = (bf16[1,512,768]{2,1,0:T(8,128)(2,1)S(1)}, bf16[1,512,768]{2,1,0:T(8,128)(2,1)}, u32[]{:S(2)}) copy-start(bf16[1,512,768]{2,1,0:T(8,128)(2,1)} %param.11) | copy-start | bytes 2359300
  10.7 104.0 %all-gather.6.cloned.1.call-start = ((), (), s32[]{:S(2)}) async-start(), calls=%async_computation.3 | async-start | bytes 5898240 | tf_op jit(solution)/shard_map/all_gather | solution.py:49
  11.5 182.1 %reduce-scatter.2.cloned.1.call-start = ((), (), s32[]{:S(2)}) async-start(), calls=%async_computation.2 | async-start | bytes 3932160 | tf_op jit(solution)/shard_map/reduce_scatter | solution.py:77
  11.5 18.0 %collective-permute-start = (bf16[512,768]{1,0:T(8,128)(2,1)S(1)}, bf16[512,768]{1,0:T(8,128)(2,1)S(1)}, u32[]{:S(2)}, u32[]{:S(2)}) collective-permute-start(bf16[512,768]{1,0:T(8,128)(2,1)S(1)} %bitcast.45), channel_id=1, source_target_pairs={{0,1},{1,2},{2,3},{3,0},{4,5},{5,6},{6,7},{7,4},{8,9},{9,10},{10,1... | collective-permute-start | bytes 2359304 | tf_op jit(solution)/shard_map/ppermute | solution.py:22
  12.1 113.5 %collective-permute-start.2 = (bf16[512,768]{1,0:T(8,128)(2,1)S(1)}, bf16[512,768]{1,0:T(8,128)(2,1)S(1)}, u32[]{:S(2)}, u32[]{:S(2)}) collective-permute-start(bf16[512,768]{1,0:T(8,128)(2,1)S(1)} %bitcast.46), channel_id=1, source_target_pairs={{0,3},{1,0},{2,1},{3,2},{4,7},{5,4},{6,5},{7,6},{8,11},{9,8},{10,9... | collective-permute-start | bytes 2359304 | tf_op jit(solution)/shard_map/ppermute | solution.py:23
  29.5 95.5 %collective-permute-start.1 = (bf16[512,768]{1,0:T(8,128)(2,1)S(1)}, bf16[512,768]{1,0:T(8,128)(2,1)S(1)}, u32[]{:S(2)}, u32[]{:S(2)}) collective-permute-start(bf16[512,768]{1,0:T(8,128)(2,1)S(1)} %collective-permute-done), channel_id=1, source_target_pairs={{0,1},{1,2},{2,3},{3,0},{4,5},{5,6},{6,7},{7,4},{8,9},{9,10},{10,1... | collective-permute-start | bytes 2359304 | tf_op jit(solution)/shard_map/ppermute | solution.py:22
  120.6 2.4 %copy-start.4 = (f32[1,128]{1,0:T(1,128)S(1)}, f32[1,128]{1,0:T(1,128)}, u32[]{:S(2)}) copy-start(f32[1,128]{1,0:T(1,128)} %param.10) | copy-start | bytes 1540
  120.6 2.4 %copy-start.5 = (f32[1,128]{1,0:T(1,128)S(1)}, f32[1,128]{1,0:T(1,128)}, u32[]{:S(2)}) copy-start(f32[1,128]{1,0:T(1,128)} %param.9) | copy-start | bytes 1540
  133.1 60.6 %copy-start.1 = (bf16[64,2,3072]{2,1,0:T(2,128)(2,1)S(1)}, bf16[64,2,3072]{2,1,0:T(2,128)(2,1)}, u32[]{:S(2)}) copy-start(bf16[64,2,3072]{2,1,0:T(2,128)(2,1)} %param.6) | copy-start | bytes 2359300
Sparse Core Ops, SparseCore 0:
  10.9 66.1 all-gather.3
  78.6 36.0 all-gather.5
  133.2 60.3 reduce-scatter.1
